TPU v7x, 32 devices: a whole 2x2x4 slice. The times are simulated.
32 devices in a mesh: rows: 8 (over y, x, core), sub: 4 (over z).
Axes of the slice: x: 2, y: 2, z: 4, core: 2. Of those that a mesh axis runs over, the one named last changes fastest.
Arguments:
- u_fem: float32 [120, 524288], P(None, ('rows', 'sub')), may hold values from -600 to 600
- resid_fem: float32 [1, 524288], P(None, ('rows', 'sub')), may hold values from -60 to 60
- slot_map: int32 [32, 32], P(('rows', 'sub')), may hold values from 0 to 31, as said below
- restart: float32 [120, 40], replicated, may hold values from -0.5 to 0.5
- coeff: float32 [3, 120, 120], P(None, None, 'sub'), may hold values from -6 to 6
Outputs:
- new_basis: float32 [40, 524288], P(None, ('rows', 'sub'))
- next_vector: float32 [1, 524288], P(None, ('rows', 'sub'))
- new_coeff: float32 [3, 40, 120], replicated
Inputs may be any that keep to these rules, and one draw needn't show every extreme that they name: Each row of slot_map is a permutation of 0 to 31.
All inputs are finite; a program needn't handle non-finite values.
Results may differ from a plain program's by a relative error of at most 0.00015.
Values sent between devices are 32-bit elements; how exact they have to be, the bound alone decides.
A program may use at most 64 MiB of HBM per device.

v0:
```python
import jax
import jax.numpy as jnp
from jax import lax
from jax.sharding import PartitionSpec as P


def settle(values, source, dev_count):
    width = values.shape[0]
    block_len = values.shape[1] // dev_count
    blocks = values.reshape(width, dev_count, block_len)
    return jnp.take(blocks, source, axis=1).reshape(width, dev_count * block_len)


def local(u_fem, resid_fem, slot_map, restart, coeff):
    highest = lax.Precision.HIGHEST
    dev_count = lax.axis_size(("rows", "sub"))
    nrows_all = u_fem.shape[1] * dev_count
    source = jnp.argsort(slot_map[0])
    basis_rows, resid_row = (u_fem, resid_fem)
    gram_local = jnp.einsum("kn,jn->kj", basis_rows, basis_rows, precision=highest)
    inner_local = jnp.einsum("kn,n->k", basis_rows, resid_row[0], precision=highest)
    gram_sum = lax.psum(gram_local, ("rows", "sub"))
    chol_lower = jnp.linalg.cholesky(gram_sum / nrows_all)
    factor = lax.linalg.triangular_solve(
        chol_lower, restart, left_side=True, lower=True, transpose_a=True
    )
    new_rows = jnp.einsum("kp,kn->pn", factor, basis_rows, precision=highest)
    inner_prod = lax.psum(inner_local, ("rows", "sub"))
    half_solve = lax.linalg.triangular_solve(
        chol_lower, inner_prod[:, None], left_side=True, lower=True
    )
    proj_coef = (
        lax.linalg.triangular_solve(
            chol_lower, half_solve, left_side=True, lower=True, transpose_a=True
        )[:, 0]
        / nrows_all
    )
    remainder = resid_row - jnp.einsum("k,kn->n", proj_coef, basis_rows, precision=highest)[None, :]
    norm_sum = lax.psum(jnp.sum(remainder * remainder), ("rows", "sub"))
    next_row = remainder * lax.rsqrt(norm_sum / nrows_all + 1e-06)
    new_rows, next_row = (
        lax.all_to_all(new_rows, ("rows", "sub"), split_axis=1, concat_axis=1, tiled=True),
        lax.all_to_all(next_row, ("rows", "sub"), split_axis=1, concat_axis=1, tiled=True),
    )
    new_rows = settle(new_rows, source, dev_count)
    next_row = settle(next_row, source, dev_count)
    raised = jnp.dot(chol_lower, restart, precision=highest)
    coeff_all = lax.all_gather(coeff, "sub", axis=2, tiled=True)
    rotated = jnp.einsum("kp,ikm->ipm", raised, coeff_all, precision=highest)
    new_coeff = rotated * lax.rsqrt(jnp.mean(rotated * rotated) + 1e-06)
    return (new_rows, next_row, new_coeff)


def solution(mesh):
    in_specs = (
        P(None, ("rows", "sub")),
        P(None, ("rows", "sub")),
        P(("rows", "sub"), None),
        P(),
        P(None, None, "sub"),
    )
    out_specs = (P(None, ("rows", "sub")), P(None, ("rows", "sub")), P())
    return jax.shard_map(local, mesh=mesh, in_specs=in_specs, out_specs=out_specs, check_vma=False)
```

profile of v0, /device:TPU:0, one launch (start us, length us, event | category | flops | bytes accessed | tf_op | source)
XLA Modules:
  0.0 229.9 jit_solution(9403381852364649270)
XLA Ops:
  0.7 10.1 %fusion.16 = f32[120,120]{0,1:T(8,128)S(1)} fusion(f32[120,16384]{1,0:T(8,128)} %param.5), kind=kOutput, calls=%fused_computation.44 | convolution fusion | flops 2831155200 | bytes 7921920 | tf_op jit(solution)/shard_map/kn,jn->kj/dot_general | solution.py:20
  10.8 6.2 %convolution_bitcast_fusion.3 = f32[120]{0:T(128)S(1)} fusion(f32[120,16384]{1,0:T(8,128)S(1)} %copy-done.1, f32[1,16384]{1,0:T(1,128)S(1)} %copy-done.2), kind=kOutput, calls=%fused_computation.10 | convolution fusion | flops 23592960 | bytes 7930336 | tf_op jit(solution)/shard_map/kn,n->k/dot_general | solution.py:21
  16.9 42.8 %all-reduce = (f32[120,120]{0,1:T(8,128)S(1)}, f32[120]{0:T(128)S(1)}) all-reduce(f32[120,120]{0,1:T(8,128)S(1)} %fusion.16, f32[120]{0:T(128)S(1)} %convolution_bitcast_fusion.3), channel_id=1, replica_groups=mesh['rows'=8,'sub'=4] {'rows','sub'}, use_global_device_ids=true, to_apply=%region_1.2 | all-reduce | flops 14520 | bytes 116160 | tf_op jit(solution)/shard_map/psum | solution.py:22
  59.9 11.0 %cholesky.16 = f32[120,120]{1,0:T(8,128)S(1)} custom-call(f32[120,120]{1,0:T(8,128)S(1)} %fusion.9), custom_call_target="Cholesky" | custom-call | tf_op jit(solution)/shard_map/jit(cholesky)/cholesky | solution.py:23
  70.9 0.6 compare_reduce_fusion
  71.5 0.7 select_bitcast_fusion
  72.2 9.2 %custom-call.10 = f32[1,120,120]{1,2,0:T(8,128)S(1)} custom-call(f32[1,120,120]{2,1,0:T(8,128)S(1)} %select_bitcast_fusion), custom_call_target="InvertDiagBlocksLowerTriangular" | custom-call | tf_op jit(solution)/shard_map/triangular_solve | solution.py:24
  81.8 6.7 %multiply_reduce_fusion = (f32[]{:T(128)}, f32[1,16384]{1,0:T(1,128)S(1)}) fusion(f32[1,16384]{1,0:T(1,128)S(1)} %copy-done.2, f32[120,1]{0,1:T(1,128)S(1)} %fusion.1, f32[120,16384]{1,0:T(8,128)} %param.5), kind=kOutput, calls=%fused_computation.15 | convolution fusion | flops 23642112 | bytes 7995876 | tf_op jit(solution)/shard_map/k,kn->n/dot_general | solution.py:38
  88.5 40.3 %psum.23 = f32[]{:T(128)} all-reduce(f32[]{:T(128)} %get-tuple-element.7), channel_id=1, replica_groups=mesh['rows'=8,'sub'=4] {'rows','sub'}, use_global_device_ids=true, to_apply=%region_6.7 | all-reduce | flops 1 | bytes 8 | tf_op jit(solution)/shard_map/psum | solution.py:39
  129.5 0.7 broadcast_multiply_fusion
  130.1 5.4 %all-to-all-start.1 = ((f32[1,32,512]{2,0,1:T(1,128)}), f32[1,32,512]{2,0,1:T(1,128)S(1)}, u32[]{:S(2)}, u32[]{:S(2)}) async-start(f32[1,32,512]{2,0,1:T(1,128)} %bitcast.14), calls=%async_computation.1 | async-start | bytes 131072 | tf_op jit(solution)/shard_map/all_to_all | solution.py:43
  135.8 6.5 %fusion.17 = f32[40,16384]{1,0:T(8,128)S(1)} fusion(f32[120,40]{0,1:T(8,128)S(1)} %fusion.7, f32[120,16384]{1,0:T(8,128)} %param.5), kind=kOutput, calls=%fused_computation.45 | convolution fusion | flops 943718400 | bytes 10504960 | tf_op jit(solution)/shard_map/kp,kn->pn/dot_general | solution.py:27
  142.3 1.7 copy.36
  144.1 1.7 sort.17
  145.8 5.8 %all-to-all-start = ((f32[40,32,512]{2,0,1:T(8,128)}), f32[40,32,512]{2,0,1:T(8,128)S(1)}, u32[]{:S(2)}, u32[]{:S(2)}) async-start(f32[40,32,512]{2,0,1:T(8,128)} %bitcast.69), calls=%async_computation | async-start | bytes 5242880 | tf_op jit(solution)/shard_map/all_to_all | solution.py:42
  151.8 67.3 %all_gather.3 = f32[3,120,120]{1,0,2:T(4,128)S(1)} all-gather(f32[3,120,30]{1,0,2:T(4,128)S(1)} %copy.21), channel_id=1, replica_groups=mesh['rows'=8,'sub'=4] {'sub'}, dimensions={2}, use_global_device_ids=true | all-gather | bytes 216000 | tf_op jit(solution)/shard_map/all_gather | solution.py:48
  219.1 0.9 convolution_bitcast_fusion
  220.0 1.0 multiply_reduce_fusion.1
  221.9 0.6 multiply_bitcast_fusion
  222.5 0.6 gather_fusion.1
  223.2 0.7 broadcast_select_fusion.1
  223.9 2.2 gather_fusion
  226.2 2.1 copy.26
  228.2 1.7 broadcast_select_fusion
  (30 shorter events, 1.1 us)
Async XLA Ops:
  0.6 134.9 %copy-start = (f32[120,40]{0,1:T(8,128)S(1)}, f32[120,40]{0,1:T(8,128)}, u32[]{:S(2)}) copy-start(f32[120,40]{0,1:T(8,128)} %param.8) | copy-start | bytes 57604
  0.6 10.1 %copy-start.1 = (f32[120,16384]{1,0:T(8,128)S(1)}, f32[120,16384]{1,0:T(8,128)}, u32[]{:S(2)}) copy-start(f32[120,16384]{1,0:T(8,128)} %param.5) | copy-start | bytes 23592964
  0.7 10.1 %copy-start.2 = (f32[1,16384]{1,0:T(1,128)S(1)}, f32[1,16384]{1,0:T(1,128)}, u32[]{:S(2)}) copy-start(f32[1,16384]{1,0:T(1,128)} %param.6) | copy-start | bytes 196612
  130.1 15.6 %all-to-all-start.1 = ((f32[1,32,512]{2,0,1:T(1,128)}), f32[1,32,512]{2,0,1:T(1,128)S(1)}, u32[]{:S(2)}, u32[]{:S(2)}) async-start(f32[1,32,512]{2,0,1:T(1,128)} %bitcast.14), calls=%async_computation.1 | async-start | bytes 131072 | tf_op jit(solution)/shard_map/all_to_all | solution.py:43
  135.8 8.3 %copy-start.4 = (s32[1,32]{1,0:T(1,128)S(1)}, s32[1,32]{1,0:T(1,128)}, u32[]{:S(2)}) copy-start(s32[1,32]{1,0:T(1,128)} %param.7) | copy-start | bytes 388
  142.3 9.4 %copy-start.3 = (f32[3,120,30]{1,2,0:T(8,128)S(1)}, f32[3,120,30]{1,2,0:T(8,128)}, u32[]{:S(2)}) copy-start(f32[3,120,30]{1,2,0:T(8,128)} %param.9) | copy-start | bytes 129604
  145.8 78.2 %all-to-all-start = ((f32[40,32,512]{2,0,1:T(8,128)}), f32[40,32,512]{2,0,1:T(8,128)S(1)}, u32[]{:S(2)}, u32[]{:S(2)}) async-start(f32[40,32,512]{2,0,1:T(8,128)} %bitcast.69), calls=%async_computation | async-start | bytes 5242880 | tf_op jit(solution)/shard_map/all_to_all | solution.py:42
where the time goes:
time: 231 us; the launch traced here: 230 us
  blocking collectives  150 us (65%)
  matrix products  32 us (14%)
  other arithmetic  27 us (12%)
  starting transfers between devices  11.2 us (5%)
  local copies, waits for them, and re-layouts  7.06 us (3%)
    all_gather x1, blocking collectives, local(): coeff_all = lax.all_gather(coeff, 'sub', axis=2, tiled=True)  67.3 us
    psum x1, blocking collectives, local(): gram_sum = lax.psum(gram_local, ('rows', 'sub'))  42.8 us
    psum x1, blocking collectives, local(): norm_sum = lax.psum(jnp.sum(remainder * remainder), ('rows', 'sub'))  40.3 us
    another operation x3, other arithmetic, local(): chol_lower = jnp.linalg.cholesky(gram_sum / nrows_all)  11.6 us
    dot_general x1, matrix products, local(): jnp.einsum('kn,jn->kj', basis_rows, basis_rows, precision=highest)  10.1 us
    another operation x2, other arithmetic, local(): lax.linalg.triangular_solve(chol_lower, restart, left_side=True, lower=Tr...  9.85 us
    dot_general x1, matrix products, local(): jnp.einsum('k,kn->n', proj_coef, basis_rows, precision=highest)[None, :]  6.74 us
    dot_general x1, matrix products, local(): new_rows = jnp.einsum('kp,kn->pn', factor, basis_rows, precision=highest)  6.51 us
  transfers between devices with their start and end apart: 2, of which 0 were waited for; matrix products, arithmetic and copies ran while one was open for 6% of the time, Pallas kernels for 0%

commit v1 on v0

v1 whole, which is shorter than its diff:
```python
import functools

import jax
import jax.numpy as jnp
from jax import lax
from jax.experimental import pallas as pl
from jax.experimental.pallas import tpu as pltpu

HIGHEST = lax.Precision.HIGHEST
MESH = pl.DeviceIdType.MESH
AXES = ("rows", "sub")
LANES = 128


def round_up(value, unit):
    return -(-value // unit) * unit


def me_of(ns):
    return lax.axis_index("rows") * ns + lax.axis_index("sub")


def greet_all(me, ndev, ns):
    barrier = pltpu.get_barrier_semaphore()

    def greet(o, carry):
        j = (me + o) % ndev
        pl.semaphore_signal(barrier, inc=1, device_id=(j // ns, j % ns), device_id_type=MESH)
        return carry

    lax.fori_loop(1, ndev, greet, 0)
    return barrier


def gram_kernel(ndev, ns, chunk, u_ref, r_ref, out_ref, stage, rs_buf, red, ag_buf, s1, r1, s2, r2):
    me = me_of(ns)
    barrier = greet_all(me, ndev, ns)
    width = out_ref.shape[1]
    pad = width - u_ref.shape[0]
    rpd = width // ndev

    def piece(c, acc):
        cols = pl.ds(pl.multiple_of(c * chunk, chunk), chunk)
        first = lax.broadcasted_iota(jnp.int32, (pad, chunk), 0) == 0
        tail = jnp.where(first, jnp.broadcast_to(r_ref[:, cols], (pad, chunk)), 0.0)
        x = jnp.concatenate([u_ref[:, cols], tail], axis=0)
        hi = x.astype(jnp.bfloat16)
        lo = (x - hi.astype(jnp.float32)).astype(jnp.bfloat16)
        both = jnp.concatenate([hi, lo], axis=0)
        return acc + lax.dot_general(both, both, (((1,), (1,)), ((), ())), preferred_element_type=jnp.float32)

    full = lax.fori_loop(0, u_ref.shape[1] // chunk, piece, jnp.zeros((2 * width, 2 * width), jnp.float32))
    cross = full[:width, width:]
    gram = full[:width, :width] + (cross + cross.T) + full[width:, width:]
    for i in range(ndev):
        stage[i] = gram[i * rpd : (i + 1) * rpd, :]
    rs_buf[me] = stage[me]
    pl.semaphore_wait(barrier, ndev - 1)

    def scatter_copy(j, slot):
        return pltpu.make_async_remote_copy(
            src_ref=stage.at[j], dst_ref=rs_buf.at[slot], send_sem=s1.at[j], recv_sem=r1.at[slot],
            device_id=(j // ns, j % ns), device_id_type=MESH)

    def gather_copy(j, slot):
        return pltpu.make_async_remote_copy(
            src_ref=red, dst_ref=ag_buf.at[slot], send_sem=s2.at[j], recv_sem=r2.at[slot],
            device_id=(j // ns, j % ns), device_id_type=MESH)

    def loop(action):
        def body(o, carry):
            action((me + o) % ndev)
            return carry
        lax.fori_loop(1, ndev, body, 0)

    loop(lambda j: scatter_copy(j, me).start())
    loop(lambda j: scatter_copy(j, j).wait_recv())
    total = jnp.sum(rs_buf[...], axis=0)
    red[...] = total
    ag_buf[me] = total
    loop(lambda j: gather_copy(j, me).start())
    loop(lambda j: gather_copy(j, j).wait_recv())
    for i in range(ndev):
        out_ref[i * rpd : (i + 1) * rpd, :] = ag_buf[i]
    loop(lambda j: scatter_copy(j, me).wait_send())
    loop(lambda j: gather_copy(j, me).wait_send())


def gram_sums(u, r, ndev, ns):
    width = LANES
    rpd = width // ndev
    chunk = min(2048, u.shape[1])
    dma = pltpu.SemaphoreType.DMA((ndev,))
    vmem = pl.BlockSpec(memory_space=pltpu.VMEM)
    return pl.pallas_call(
        functools.partial(gram_kernel, ndev, ns, chunk),
        out_shape=jax.ShapeDtypeStruct((width, width), jnp.float32),
        in_specs=[vmem, vmem],
        out_specs=vmem,
        scratch_shapes=[
            pltpu.VMEM((ndev, rpd, width), jnp.float32),
            pltpu.VMEM((ndev, rpd, width), jnp.float32),
            pltpu.VMEM((rpd, width), jnp.float32),
            pltpu.VMEM((ndev, rpd, width), jnp.float32),
            dma, dma, dma, dma,
        ],
        compiler_params=pltpu.CompilerParams(
            collective_id=0, has_side_effects=True, vmem_limit_bytes=40 * 1024 * 1024),
    )(u, r)


def exchange_kernel(ndev, ns, keep, count, u_ref, r_ref, w_ref, raised_ref, coeff_ref,
                    big_out, small_out, coeff_out, send, small, cg, own_sem,
                    s1, r1, s2, r2, s3, r3):
    r, s = lax.axis_index("rows"), lax.axis_index("sub")
    me = r * ns + s
    nr = ndev // ns
    bs = send.shape[2]
    barrier = greet_all(me, ndev, ns)

    def coeff_copy(t, slot):
        return pltpu.make_async_remote_copy(
            src_ref=coeff_ref, dst_ref=cg.at[slot], send_sem=s3.at[t], recv_sem=r3.at[slot],
            device_id=(r, t), device_id_type=MESH)

    def big_copy(j, slot):
        return pltpu.make_async_remote_copy(
            src_ref=send.at[j], dst_ref=big_out.at[slot], send_sem=s1.at[j], recv_sem=r1.at[slot],
            device_id=(j // ns, j % ns), device_id_type=MESH)

    def small_copy(j, slot):
        return pltpu.make_async_remote_copy(
            src_ref=small.at[j], dst_ref=small_out.at[slot], send_sem=s2.at[j], recv_sem=r2.at[slot],
            device_id=(j // ns, j % ns), device_id_type=MESH)

    def loop(action):
        def body(o, carry):
            action((me + o) % ndev)
            return carry
        lax.fori_loop(1, ndev, body, 0)

    weights = w_ref[...]
    half = ns // 2
    side, pos = s // half, s % half
    across = [(1 - side) * half + (pos + q) % half for q in range(half)]
    beside = [side * half + (pos + q) % half for q in range(half)]
    order = []
    for q in range(half):
        order += [across[q], beside[half - 1 - q]]

    def step(d, acc):
        targets = [((r + d) % nr) * ns + t for t in order]
        for j in targets:
            cols = pl.ds(pl.multiple_of(j * bs, bs), bs)
            y = jnp.dot(weights, u_ref[:, cols], precision=HIGHEST, preferred_element_type=jnp.float32)
            rest = r_ref[:, cols] - y[keep : keep + 1, :]
            send[j] = y[:keep, :]
            small[j, 0:1, :] = rest
            acc = acc + rest * rest

        @pl.when(d == 0)
        def _():
            pl.semaphore_wait(barrier, ndev - 1)

        for j in targets:
            @pl.when(j != me)
            def _():
                big_copy(j, me).start()

        return acc

    acc = lax.fori_loop(0, nr, step, jnp.zeros((1, bs), jnp.float32))
    partial = jnp.sum(acc, axis=1, keepdims=True)

    def mark(j, carry):
        small[j, 1:2, :] = jnp.broadcast_to(partial, (1, bs))
        return carry

    lax.fori_loop(0, ndev, mark, 0)
    own_big = pltpu.make_async_copy(send.at[me], big_out.at[me], own_sem.at[0])
    own_small = pltpu.make_async_copy(small.at[me], small_out.at[me], own_sem.at[1])
    own_big.start()
    own_small.start()
    for o in range(1, ns):
        coeff_copy((s + o) % ns, s).start()
    loop(lambda j: small_copy(j, me).start())
    cg[s] = coeff_ref[...]
    for o in range(1, ns):
        coeff_copy((s + o) % ns, (s + o) % ns).wait_recv()
    turned = [
        lax.dot_general(raised_ref[...], cg[t], (((1,), (1,)), ((), ())), precision=HIGHEST,
                        preferred_element_type=jnp.float32)
        for t in range(ns)
    ]
    squares = sum(jnp.sum(part * part) for part in turned)
    scale = lax.rsqrt(jnp.full((1, 1), squares / count + 1e-06, jnp.float32))
    for t in range(ns):
        coeff_out[t] = turned[t] * scale
    own_big.wait()
    own_small.wait()
    loop(lambda j: big_copy(j, j).wait_recv())
    loop(lambda j: small_copy(j, j).wait_recv())
    loop(lambda j: big_copy(j, me).wait_send())
    loop(lambda j: small_copy(j, me).wait_send())
    for o in range(1, ns):
        coeff_copy((s + o) % ns, s).wait_send()


def exchange(u, r, weights, raised, coeff_t, keep, count, ndev, ns):
    bs = u.shape[1] // ndev
    vmem = pl.BlockSpec(memory_space=pltpu.VMEM)
    hbm = pl.BlockSpec(memory_space=pl.ANY)
    dma = pltpu.SemaphoreType.DMA((ndev,))
    few = pltpu.SemaphoreType.DMA((ns,))
    f32 = jnp.float32
    return pl.pallas_call(
        functools.partial(exchange_kernel, ndev, ns, keep, count),
        out_shape=(
            jax.ShapeDtypeStruct((ndev, keep, bs), f32),
            jax.ShapeDtypeStruct((ndev, 2, bs), f32),
            jax.ShapeDtypeStruct((ns, keep, coeff_t.shape[0]), f32),
        ),
        in_specs=[vmem] * 5,
        out_specs=(hbm, hbm, vmem),
        scratch_shapes=[
            pltpu.VMEM((ndev, keep, bs), f32),
            pltpu.VMEM((ndev, 2, bs), f32),
            pltpu.VMEM((ns,) + coeff_t.shape, f32),
            pltpu.SemaphoreType.DMA((2,)),
            dma, dma, dma, dma, few, few,
        ],
        compiler_params=pltpu.CompilerParams(
            collective_id=1, has_side_effects=True, vmem_limit_bytes=40 * 1024 * 1024),
    )(u, r, weights, raised, coeff_t)


def place_kernel(ndev, nrows, slots, big, small, rows_out, vec_out, held, in_sem, out_sem):
    bs = held.shape[2]

    def fetch(d):
        return pltpu.make_async_copy(big.at[d], held.at[d], in_sem.at[d])

    def put(d):
        cols = pl.ds(pl.multiple_of(slots[0, d] * bs, bs), bs)
        return pltpu.make_async_copy(held.at[d], rows_out.at[:, cols], out_sem.at[d])

    def loop(action):
        def body(d, carry):
            action(d)
            return carry
        lax.fori_loop(0, ndev, body, 0)

    loop(lambda d: fetch(d).start())
    total = jnp.sum(small[:, 1, :], axis=0, keepdims=True)
    scale = lax.rsqrt(total / nrows + 1e-06)

    def move(d):
        fetch(d).wait()
        put(d).start()
        cols = pl.ds(pl.multiple_of(slots[0, d] * bs, bs), bs)
        vec_out[:, cols] = small[d, 0:1, :] * scale

    loop(move)
    loop(lambda d: put(d).wait())


def place(slot_row, big, small, nrows):
    ndev, keep, bs = big.shape
    vmem = pl.BlockSpec(memory_space=pltpu.VMEM)
    hbm = pl.BlockSpec(memory_space=pl.ANY)
    dma = pltpu.SemaphoreType.DMA((ndev,))
    return pl.pallas_call(
        functools.partial(place_kernel, ndev, nrows),
        out_shape=(
            jax.ShapeDtypeStruct((keep, ndev * bs), jnp.float32),
            jax.ShapeDtypeStruct((1, ndev * bs), jnp.float32),
        ),
        in_specs=[pl.BlockSpec(memory_space=pltpu.SMEM), hbm, vmem],
        out_specs=(hbm, vmem),
        scratch_shapes=[pltpu.VMEM((ndev, keep, bs), jnp.float32), dma, dma],
        compiler_params=pltpu.CompilerParams(vmem_limit_bytes=20 * 1024 * 1024),
    )(slot_row, big, small)


def small_algebra(sums, restart, nrows):
    k = restart.shape[0]
    lower = jnp.linalg.cholesky(sums[:k, :k] / nrows)
    inner = sums[:k, k : k + 1]
    factor = lax.linalg.triangular_solve(lower, restart, left_side=True, lower=True, transpose_a=True)
    half_solve = lax.linalg.triangular_solve(lower, inner, left_side=True, lower=True)
    proj = lax.linalg.triangular_solve(lower, half_solve, left_side=True, lower=True, transpose_a=True) / nrows
    keep = restart.shape[1]
    weights = jnp.concatenate([factor, proj], axis=1).T
    weights = jnp.pad(weights, ((0, round_up(keep + 1, 8) - keep - 1), (0, 0)))
    raised = jnp.dot(lower, restart, precision=HIGHEST)
    return weights, raised.T


def local(u, r, slot_map, restart, coeff):
    ndev = lax.axis_size(AXES)
    ns = lax.axis_size("sub")
    k, keep = restart.shape
    nrows = u.shape[1] * ndev
    deg, _, mloc = coeff.shape
    sums = gram_sums(u, r, ndev, ns)
    weights, raised = small_algebra(sums, restart, nrows)
    coeff_t = coeff.transpose(0, 2, 1).reshape(deg * mloc, k)
    tall = round_up(deg * mloc, 8)
    coeff_t = jnp.pad(coeff_t, ((0, tall - deg * mloc), (0, 0)))
    big, small, turned = exchange(u, r, weights, raised, coeff_t, keep, deg * keep * mloc * ns, ndev, ns)
    rows, vec = place(slot_map, big, small, nrows)
    turned = turned[:, :, : deg * mloc].reshape(ns, keep, deg, mloc)
    new_coeff = turned.transpose(2, 1, 0, 3).reshape(deg, keep, ns * mloc)
    return rows, vec, new_coeff


def solution(mesh):
    P = jax.sharding.PartitionSpec
    in_specs = (P(None, AXES), P(None, AXES), P(AXES, None), P(), P(None, None, "sub"))
    out_specs = (P(None, AXES), P(None, AXES), P())
    return jax.shard_map(local, mesh=mesh, in_specs=in_specs, out_specs=out_specs, check_vma=False)
```

time: 231 us -> 130 us (0.56)
  blocking collectives: 150 us -> 0 us
  Pallas kernels: 0 us -> 96.7 us
  matrix products: 32 us -> 1.52 us
  starting transfers between devices: 11.2 us -> 0 us
  other arithmetic: 27 us -> 21.5 us
  local copies, waits for them, and re-layouts: 7.06 us -> 9.58 us
    pallas_call x0 -> x3, Pallas kernels: none -> 96.7 us  [the longest x1 71.3 us: exchange(): pl.pallas_call(functools.partial(exchange_kernel, ndev, ns, keep, count),...]
    psum x2 -> x0, blocking collectives: 83.1 us -> none  [the longest x1 42.8 us: local(): gram_sum = lax.psum(gram_local, ('rows', 'sub'))]
    all_gather x1 -> x0, blocking collectives: 67.3 us -> none  [local(): coeff_all = lax.all_gather(coeff, 'sub', axis=2, tiled=True)]
    dot_general x6 -> x1, matrix products: 31.4 us -> 0.89 us  [small_algebra(): raised = jnp.dot(lower, restart, precision=HIGHEST)]
    all_to_all x2 -> x0, starting transfers between devices: 11.2 us -> none  [the longest x1 5.83 us: local(): lax.all_to_all(new_rows, ('rows', 'sub'), split_axis=1, concat_axis=1, ti...]
    unnamed x17 -> x13, local copies, waits for them, and re-layouts: 0.38 us -> 7.4 us
    gather x3 -> x0, local copies, waits for them, and re-layouts: 4.86 us -> none  [settle(): jnp.take(blocks, source, axis=1).reshape(width, dev_count * block_len)]
    select_n x3 -> x0, other arithmetic: 2.44 us -> none  [settle(): jnp.take(blocks, source, axis=1).reshape(width, dev_count * block_len)]
  transfers between devices with their start and end apart: 2 -> 0, of which waited for: 0 -> 0; matrix products, arithmetic and copies ran while one was open for 6% -> 0% of each run, Pallas kernels for 0% -> 0%
where the time goes in v1:
time: 130 us
  Pallas kernels  96.7 us (74%)
  other arithmetic  21.5 us (17%)
  local copies, waits for them, and re-layouts  9.58 us (7%)
  matrix products  1.52 us (1%)
    pallas_call x1, Pallas kernels, exchange(): pl.pallas_call(functools.partial(exchange_kernel, ndev, ns, keep, count),...  71.3 us
    pallas_call x1, Pallas kernels, gram_sums(): pl.pallas_call(functools.partial(gram_kernel, ndev, ns, chunk), out_shape...  18.5 us
    another operation x3, other arithmetic, small_algebra(): lower = jnp.linalg.cholesky(sums[:k, :k] / nrows)  11.6 us
    another operation x2, other arithmetic, small_algebra(): lax.linalg.triangular_solve(lower, restart, left_side=True, lower=True, t...  9.86 us
    unnamed x13, local copies, waits for them, and re-layouts  7.4 us
    pallas_call x1, Pallas kernels, place(): pl.pallas_call(functools.partial(place_kernel, ndev, nrows), out_shape=(j...  6.8 us

profile of v1, /device:TPU:0, one launch (start us, length us, event | category | flops | bytes accessed | tf_op | source)
XLA Modules:
  0.0 130.1 jit_solution(7118847980403155881)
XLA Ops:
  0.6 0.0 copy-start
  0.6 0.8 reshape.37
  1.5 0.0 copy-start.1
  1.5 3.2 %copy-done.1 = f32[120,16384]{1,0:T(8,128)S(1)} copy-done((f32[120,16384]{1,0:T(8,128)S(1)}, f32[120,16384]{1,0:T(8,128)}, u32[]{:S(2)}) %copy-start.1) | copy-done | bytes 7864344
  4.7 0.8 copy-done.3
  5.5 18.5 %shard_map.76 = f32[128,128]{1,0:T(8,128)S(1)} custom-call(f32[120,16384]{1,0:T(8,128)S(1)} %copy-done.1, f32[1,16384]{1,0:T(1,128)S(1)} %copy-done.3), custom_call_target="tpu_custom_call" | custom-call | tf_op jit(solution)/shard_map/pallas_call | solution.py:95
  24.1 0.2 slice_reduce_fusion
  24.3 0.1 copy.15
  24.4 0.1 copy.12
  24.5 11.0 %cholesky.16 = f32[120,120]{1,0:T(8,128)S(1)} custom-call(f32[120,120]{1,0:T(8,128)S(1)} %fusion.6), custom_call_target="Cholesky" | custom-call | tf_op jit(solution)/shard_map/jit(cholesky)/cholesky | solution.py:287
  35.5 0.6 compare_reduce_fusion
  36.2 0.9 convolution_bitcast_fusion.raised_ref
  37.1 0.7 select_bitcast_fusion
  37.7 9.2 %custom-call.10 = f32[1,120,120]{1,2,0:T(8,128)S(1)} custom-call(f32[1,120,120]{2,1,0:T(8,128)S(1)} %select_bitcast_fusion), custom_call_target="InvertDiagBlocksLowerTriangular" | custom-call | tf_op jit(solution)/shard_map/triangular_solve | solution.py:289
  46.9 0.2 convolution_bitcast_fusion.2
  47.1 0.2 fusion.1
  47.3 0.3 fusion.4
  47.6 0.0 copy-start.2
  47.6 3.2 %copy-done.2 = f32[120,16384]{1,0:T(8,128)S(1)} copy-done((f32[120,16384]{1,0:T(8,128)S(1)}, f32[120,16384]{1,0:T(8,128)}, u32[]{:S(2)}) %copy-start.2) | copy-done | bytes 7864344
  50.9 71.3 %shard_map.77 = (f32[32,40,512]{2,1,0:T(8,128)S(1)}, f32[32,2,512]{2,1,0:T(2,128)S(1)}, f32[4,40,96]{2,1,0:T(8,128)S(1)}) custom-call(f32[120,16384]{1,0:T(8,128)S(1)} %copy-done.2, f32[1,16384]{1,0:T(1,128)S(1)} %copy-done.4, f32[48,120]{1,0:T(8,128)S(1)} %pad.8.w_ref, f32[40,120]{1,0:T(8,128)S(1)} %convolution_bitcast_fusion.raised_ref, ...), custom_call_target="tpu_custom_call" | custom-call | tf_op jit(solution)/shard_map/pallas_call | solution.py:216
  122.2 6.8 %shard_map.78 = (f32[40,16384]{1,0:T(8,128)}, f32[1,16384]{1,0:T(1,128)}) custom-call(s32[1,32]{1,0:T(1,128)S(1)} %copy-done.5, f32[32,40,512]{2,1,0:T(8,128)S(1)} %get-tuple-element.8.big, f32[32,2,512]{2,1,0:T(2,128)S(1)} %get-tuple-element.9.small), custom_call_target="tpu_custom_call" | custom-call | tf_op jit(solution)/shard_map/pallas_call | solution.py:272
  129.0 0.1 copy.13
  129.1 0.2 copy.14
  129.3 0.8 reshape.39
  (13 shorter events, 0.1 us)
Async XLA Ops:
  0.6 35.5 %copy-start = (f32[120,40]{0,1:T(8,128)S(1)}, f32[120,40]{0,1:T(8,128)}, u32[]{:S(2)}) copy-start(f32[120,40]{0,1:T(8,128)} %param.8) | copy-start | bytes 57604
  1.5 3.2 %copy-start.1 = (f32[120,16384]{1,0:T(8,128)S(1)}, f32[120,16384]{1,0:T(8,128)}, u32[]{:S(2)}) copy-start(f32[120,16384]{1,0:T(8,128)} %u_ref.3) | copy-start | bytes 23592964
  4.7 0.8 copy-start.3
  5.5 42.1 %copy-start.4 = (f32[1,16384]{1,0:T(1,128)S(1)}, f32[1,16384]{1,0:T(1,128)}, u32[]{:S(2)}) copy-start(f32[1,16384]{1,0:T(1,128)} %r_ref.3) | copy-start | bytes 196612
  47.6 3.2 %copy-start.2 = (f32[120,16384]{1,0:T(8,128)S(1)}, f32[120,16384]{1,0:T(8,128)}, u32[]{:S(2)}) copy-start(f32[120,16384]{1,0:T(8,128)} %u_ref.3) | copy-start | bytes 23592964
  50.9 71.3 %copy-start.5 = (s32[1,32]{1,0:T(1,128)S(1)}, s32[1,32]{1,0:T(1,128)}, u32[]{:S(2)}) copy-start(s32[1,32]{1,0:T(1,128)} %slots.1) | copy-start | bytes 388

commit v2 on v1

--- a/solution.py
+++ b/solution.py
@@ -32,15 +32,25 @@
     return barrier
 
 
-def gram_kernel(ndev, ns, chunk, u_ref, r_ref, out_ref, stage, rs_buf, red, ag_buf, s1, r1, s2, r2):
+def gram_kernel(ndev, ns, chunk, u_hbm, r_hbm, out_ref, u_ref, r_ref, stage, rs_buf, red, ag_buf,
+                in_sem, s1, r1, s2, r2):
     me = me_of(ns)
+    pieces = u_ref.shape[1] // chunk
+    load_r = pltpu.make_async_copy(r_hbm, r_ref, in_sem.at[pieces])
+    load_r.start()
+    loads = []
+    for c in range(pieces):
+        cols = pl.ds(c * chunk, chunk)
+        loads.append(pltpu.make_async_copy(u_hbm.at[:, cols], u_ref.at[:, cols], in_sem.at[c]))
+        loads[-1].start()
     barrier = greet_all(me, ndev, ns)
     width = out_ref.shape[1]
     pad = width - u_ref.shape[0]
     rpd = width // ndev
 
     def piece(c, acc):
-        cols = pl.ds(pl.multiple_of(c * chunk, chunk), chunk)
+        loads[c].wait()
+        cols = pl.ds(c * chunk, chunk)
         first = lax.broadcasted_iota(jnp.int32, (pad, chunk), 0) == 0
         tail = jnp.where(first, jnp.broadcast_to(r_ref[:, cols], (pad, chunk)), 0.0)
         x = jnp.concatenate([u_ref[:, cols], tail], axis=0)
@@ -49,7 +59,10 @@
         both = jnp.concatenate([hi, lo], axis=0)
         return acc + lax.dot_general(both, both, (((1,), (1,)), ((), ())), preferred_element_type=jnp.float32)
 
-    full = lax.fori_loop(0, u_ref.shape[1] // chunk, piece, jnp.zeros((2 * width, 2 * width), jnp.float32))
+    load_r.wait()
+    full = jnp.zeros((2 * width, 2 * width), jnp.float32)
+    for c in range(pieces):
+        full = piece(c, full)
     cross = full[:width, width:]
     gram = full[:width, :width] + (cross + cross.T) + full[width:, width:]
     for i in range(ndev):
@@ -92,30 +105,80 @@
     chunk = min(2048, u.shape[1])
     dma = pltpu.SemaphoreType.DMA((ndev,))
     vmem = pl.BlockSpec(memory_space=pltpu.VMEM)
+    hbm = pl.BlockSpec(memory_space=pltpu.MemorySpace.HBM)
     return pl.pallas_call(
         functools.partial(gram_kernel, ndev, ns, chunk),
         out_shape=jax.ShapeDtypeStruct((width, width), jnp.float32),
-        in_specs=[vmem, vmem],
+        in_specs=[hbm, hbm],
         out_specs=vmem,
         scratch_shapes=[
+            pltpu.VMEM(u.shape, jnp.float32),
+            pltpu.VMEM(r.shape, jnp.float32),
             pltpu.VMEM((ndev, rpd, width), jnp.float32),
             pltpu.VMEM((ndev, rpd, width), jnp.float32),
             pltpu.VMEM((rpd, width), jnp.float32),
             pltpu.VMEM((ndev, rpd, width), jnp.float32),
+            pltpu.SemaphoreType.DMA((u.shape[1] // chunk + 1,)),
             dma, dma, dma, dma,
         ],
         compiler_params=pltpu.CompilerParams(
-            collective_id=0, has_side_effects=True, vmem_limit_bytes=40 * 1024 * 1024),
+            collective_id=0, has_side_effects=True, vmem_limit_bytes=60 * 1024 * 1024),
     )(u, r)
 
 
-def exchange_kernel(ndev, ns, keep, count, u_ref, r_ref, w_ref, raised_ref, coeff_ref,
-                    big_out, small_out, coeff_out, send, small, cg, own_sem,
+def factor_panels(sums_ref, restart_ref, work, upper, nrows, panel):
+    k, keep = restart_ref.shape
+    width = sums_ref.shape[1]
+    row = lax.broadcasted_iota(jnp.int32, (width, width), 0)
+    lane = lax.broadcasted_iota(jnp.int32, (width, width), 1)
+    line = lax.broadcasted_iota(jnp.int32, (1, width), 1)
+    work[:, :width] = sums_ref[...] * (1.0 / nrows)
+    work[:, width:] = jnp.where(row == lane, 1.0, 0.0)
+    upper[...] = jnp.zeros_like(upper)
+
+    def step(i, carry):
+        base = i * panel
+        rows = [work[pl.ds(base + a, 1), :] for a in range(panel)]
+        left = work[:, :width]
+        cols = [jnp.sum(jnp.where(lane == base + a, left, 0.0), axis=1, keepdims=True) for a in range(panel)]
+        block = {
+            (a, b): jnp.sum(jnp.where(line == base + b, rows[a][:, :width], 0.0), axis=1, keepdims=True)
+            for a in range(panel) for b in range(a, panel)
+        }
+        for a in range(panel):
+            inverse = 1.0 / block[a, a]
+            for b in range(a + 1, panel):
+                ratio = block[a, b] * inverse
+                rows[b] = rows[b] - ratio * rows[a]
+                cols[b] = cols[b] - ratio * cols[a]
+                for c in range(b, panel):
+                    block[b, c] = block[b, c] - ratio * block[a, c]
+            cols[a] = (cols[a], inverse)
+            upper[pl.ds(base + a, 1), :] = rows[a] * lax.rsqrt(block[a, a])
+        work[...] = work[...] - sum((cols[a][0] * cols[a][1]) * rows[a] for a in range(panel))
+        return carry
+
+    lax.fori_loop(0, k // panel, step, 0)
+    turned = restart_ref[...].T
+    both = jnp.dot(turned, upper[:k, :], precision=HIGHEST, preferred_element_type=jnp.float32)
+    half = upper[:, :width].T[k : k + 8, :]
+    proj = jnp.dot(half, upper[:, width:], precision=HIGHEST, preferred_element_type=jnp.float32)
+    raised = both[:, :k]
+    weights = jnp.concatenate([both[:, width:], proj], axis=0)[:, :k]
+    return weights, raised
+
+
+def exchange_kernel(ndev, ns, keep, count, nrows, u_hbm, r_hbm, sums_ref, restart_ref, coeff_ref,
+                    big_out, small_out, coeff_out, u_ref, r_ref, work, upper, load_sem, send, small, cg, own_sem,
                     s1, r1, s2, r2, s3, r3):
     r, s = lax.axis_index("rows"), lax.axis_index("sub")
     me = r * ns + s
     nr = ndev // ns
     bs = send.shape[2]
+    load_u = pltpu.make_async_copy(u_hbm, u_ref, load_sem.at[0])
+    load_r = pltpu.make_async_copy(r_hbm, r_ref, load_sem.at[1])
+    load_u.start()
+    load_r.start()
     barrier = greet_all(me, ndev, ns)
 
     def coeff_copy(t, slot):
@@ -139,7 +202,10 @@
             return carry
         lax.fori_loop(1, ndev, body, 0)
 
-    weights = w_ref[...]
+    panel = next(p for p in (4, 2, 1) if restart_ref.shape[0] % p == 0)
+    weights, raised = factor_panels(sums_ref, restart_ref, work, upper, nrows, panel)
+    load_u.wait()
+    load_r.wait()
     half = ns // 2
     side, pos = s // half, s % half
     across = [(1 - side) * half + (pos + q) % half for q in range(half)]
@@ -188,7 +254,7 @@
     for o in range(1, ns):
         coeff_copy((s + o) % ns, (s + o) % ns).wait_recv()
     turned = [
-        lax.dot_general(raised_ref[...], cg[t], (((1,), (1,)), ((), ())), precision=HIGHEST,
+        lax.dot_general(raised, cg[t], (((1,), (1,)), ((), ())), precision=HIGHEST,
                         preferred_element_type=jnp.float32)
         for t in range(ns)
     ]
@@ -206,23 +272,28 @@
         coeff_copy((s + o) % ns, s).wait_send()
 
 
-def exchange(u, r, weights, raised, coeff_t, keep, count, ndev, ns):
+def exchange(u, r, sums, restart, coeff_t, keep, count, ndev, ns):
     bs = u.shape[1] // ndev
     vmem = pl.BlockSpec(memory_space=pltpu.VMEM)
-    hbm = pl.BlockSpec(memory_space=pl.ANY)
+    hbm = pl.BlockSpec(memory_space=pltpu.MemorySpace.HBM)
     dma = pltpu.SemaphoreType.DMA((ndev,))
     few = pltpu.SemaphoreType.DMA((ns,))
     f32 = jnp.float32
     return pl.pallas_call(
-        functools.partial(exchange_kernel, ndev, ns, keep, count),
+        functools.partial(exchange_kernel, ndev, ns, keep, count, u.shape[1] * ndev),
         out_shape=(
             jax.ShapeDtypeStruct((ndev, keep, bs), f32),
             jax.ShapeDtypeStruct((ndev, 2, bs), f32),
             jax.ShapeDtypeStruct((ns, keep, coeff_t.shape[0]), f32),
         ),
-        in_specs=[vmem] * 5,
+        in_specs=[hbm, hbm, vmem, vmem, vmem],
         out_specs=(hbm, hbm, vmem),
         scratch_shapes=[
+            pltpu.VMEM(u.shape, f32),
+            pltpu.VMEM(r.shape, f32),
+            pltpu.VMEM((sums.shape[0], 2 * sums.shape[1]), f32),
+            pltpu.VMEM((sums.shape[0], 2 * sums.shape[1]), f32),
+            pltpu.SemaphoreType.DMA((2,)),
             pltpu.VMEM((ndev, keep, bs), f32),
             pltpu.VMEM((ndev, 2, bs), f32),
             pltpu.VMEM((ns,) + coeff_t.shape, f32),
@@ -230,8 +301,8 @@
             dma, dma, dma, dma, few, few,
         ],
         compiler_params=pltpu.CompilerParams(
-            collective_id=1, has_side_effects=True, vmem_limit_bytes=40 * 1024 * 1024),
-    )(u, r, weights, raised, coeff_t)
+            collective_id=1, has_side_effects=True, vmem_limit_bytes=60 * 1024 * 1024),
+    )(u, r, sums, restart, coeff_t)
 
 
 def place_kernel(ndev, nrows, slots, big, small, rows_out, vec_out, held, in_sem, out_sem):
@@ -282,20 +353,6 @@
     )(slot_row, big, small)
 
 
-def small_algebra(sums, restart, nrows):
-    k = restart.shape[0]
-    lower = jnp.linalg.cholesky(sums[:k, :k] / nrows)
-    inner = sums[:k, k : k + 1]
-    factor = lax.linalg.triangular_solve(lower, restart, left_side=True, lower=True, transpose_a=True)
-    half_solve = lax.linalg.triangular_solve(lower, inner, left_side=True, lower=True)
-    proj = lax.linalg.triangular_solve(lower, half_solve, left_side=True, lower=True, transpose_a=True) / nrows
-    keep = restart.shape[1]
-    weights = jnp.concatenate([factor, proj], axis=1).T
-    weights = jnp.pad(weights, ((0, round_up(keep + 1, 8) - keep - 1), (0, 0)))
-    raised = jnp.dot(lower, restart, precision=HIGHEST)
-    return weights, raised.T
-
-
 def local(u, r, slot_map, restart, coeff):
     ndev = lax.axis_size(AXES)
     ns = lax.axis_size("sub")
@@ -303,11 +360,10 @@
     nrows = u.shape[1] * ndev
     deg, _, mloc = coeff.shape
     sums = gram_sums(u, r, ndev, ns)
-    weights, raised = small_algebra(sums, restart, nrows)
     coeff_t = coeff.transpose(0, 2, 1).reshape(deg * mloc, k)
     tall = round_up(deg * mloc, 8)
     coeff_t = jnp.pad(coeff_t, ((0, tall - deg * mloc), (0, 0)))
-    big, small, turned = exchange(u, r, weights, raised, coeff_t, keep, deg * keep * mloc * ns, ndev, ns)
+    big, small, turned = exchange(u, r, sums, restart, coeff_t, keep, deg * keep * mloc * ns, ndev, ns)
     rows, vec = place(slot_map, big, small, nrows)
     turned = turned[:, :, : deg * mloc].reshape(ns, keep, deg, mloc)
     new_coeff = turned.transpose(2, 1, 0, 3).reshape(deg, keep, ns * mloc)

time: 130 us -> 113 us (0.87)
  other arithmetic: 21.5 us -> 0 us
  Pallas kernels: 96.7 us -> 106 us
  local copies, waits for them, and re-layouts: 9.58 us -> 6.62 us
  matrix products: 1.52 us -> 0 us
    another operation x5 -> x0, other arithmetic: 21.5 us -> none  [the longest x3 11.6 us: small_algebra(): lower = jnp.linalg.cholesky(sums[:k, :k] / nrows)]
    pallas_call x1, Pallas kernels: 71.3 us -> 77.4 us  [exchange(): pl.pallas_call(functools.partial(exchange_kernel, ndev, ns, keep, count,...]
    unnamed x13 -> x9, local copies, waits for them, and re-layouts: 7.4 us -> 4.09 us
    pallas_call x1, Pallas kernels: 18.5 us -> 21.3 us  [gram_sums(): pl.pallas_call(functools.partial(gram_kernel, ndev, ns, chunk), out_shape...]
where the time goes in v2:
time: 113 us
  Pallas kernels  106 us (94%)
  local copies, waits for them, and re-layouts  6.62 us (6%)
    pallas_call x1, Pallas kernels, exchange(): pl.pallas_call(functools.partial(exchange_kernel, ndev, ns, keep, count,...  77.4 us
    pallas_call x1, Pallas kernels, gram_sums(): pl.pallas_call(functools.partial(gram_kernel, ndev, ns, chunk), out_shape...  21.3 us
    pallas_call x1, Pallas kernels, place(): pl.pallas_call(functools.partial(place_kernel, ndev, nrows), out_shape=(j...  6.8 us
    unnamed x9, local copies, waits for them, and re-layouts  4.09 us

profile of v2, /device:TPU:0, one launch (start us, length us, event | category | flops | bytes accessed | tf_op | source)
XLA Modules:
  0.0 112.9 jit_solution(2672222955717756621)
XLA Ops:
  0.6 0.8 reshape.15
  1.4 0.6 pad.4.coeff_ref
  2.1 1.4 %copy.10.restart_ref = f32[120,40]{1,0:T(8,128)} copy(f32[120,40]{0,1:T(8,128)} %param.8) | data formatting | bytes 38400 | tf_op args[3]
  3.5 21.3 %shard_map.76.sums_ref = f32[128,128]{1,0:T(8,128)} custom-call(f32[120,16384]{1,0:T(8,128)} %u_hbm.3, f32[1,16384]{1,0:T(1,128)} %r_hbm.3), custom_call_target="tpu_custom_call" | custom-call | tf_op jit(solution)/shard_map/pallas_call | solution.py:109
  24.9 0.0 copy-start.2
  24.9 77.4 %shard_map.77 = (f32[32,40,512]{2,1,0:T(8,128)}, f32[32,2,512]{2,1,0:T(2,128)}, f32[4,40,96]{2,1,0:T(8,128)}) custom-call(f32[120,16384]{1,0:T(8,128)} %u_hbm.3, f32[1,16384]{1,0:T(1,128)} %r_hbm.3, f32[128,128]{1,0:T(8,128)} %shard_map.76.sums_ref, f32[120,40]{1,0:T(8,128)} %copy.10.restart_ref, f32[96,120]{1,0:T(8,128)} %pad.4.coeff_ref), custom_call_target="tpu_custom_call" | custom-call | tf_op jit(solution)/shard_map/pallas_call | solution.py:282
  102.3 0.0 copy-done.2
  102.3 0.0 copy-start
  102.4 1.7 %copy-done = f32[32,40,512]{2,1,0:T(8,128)S(1)} copy-done((f32[32,40,512]{2,1,0:T(8,128)S(1)}, f32[32,40,512]{2,1,0:T(8,128)}, u32[]{:S(2)}) %copy-start) | copy-done | bytes 2621464
  104.1 0.0 copy-start.1
  104.1 0.9 copy-done.1
  105.0 0.0 copy-start.3
  105.0 6.8 %shard_map.78 = (f32[40,16384]{1,0:T(8,128)}, f32[1,16384]{1,0:T(1,128)}) custom-call(s32[1,32]{1,0:T(1,128)S(1)} %copy-done.2, f32[32,40,512]{2,1,0:T(8,128)S(1)} %copy-done, f32[32,2,512]{2,1,0:T(2,128)S(1)} %copy-done.1), custom_call_target="tpu_custom_call" | custom-call | tf_op jit(solution)/shard_map/pallas_call | solution.py:343
  111.8 0.0 copy-done.3
  111.8 0.1 copy.11
  111.9 0.2 copy.12
  112.1 0.8 reshape.17
Async XLA Ops:
  24.9 77.5 %copy-start.2 = (s32[1,32]{1,0:T(1,128)S(1)}, s32[1,32]{1,0:T(1,128)}, u32[]{:S(2)}) copy-start(s32[1,32]{1,0:T(1,128)} %slots.1) | copy-start | bytes 388
  102.3 1.7 %copy-start = (f32[32,40,512]{2,1,0:T(8,128)S(1)}, f32[32,40,512]{2,1,0:T(8,128)}, u32[]{:S(2)}) copy-start(f32[32,40,512]{2,1,0:T(8,128)} %get-tuple-element.8.big) | copy-start | bytes 7864324
  104.1 0.9 copy-start.1
  105.0 6.8 %copy-start.3 = (f32[4,40,96]{2,1,0:T(8,128)S(1)}, f32[4,40,96]{2,1,0:T(8,128)}, u32[]{:S(2)}) copy-start(f32[4,40,96]{2,1,0:T(8,128)} %get-tuple-element.12) | copy-start | bytes 184324

commit v3 on v2

--- a/solution.py
+++ b/solution.py
@@ -10,10 +10,6 @@
 MESH = pl.DeviceIdType.MESH
 AXES = ("rows", "sub")
 LANES = 128
-
-
-def round_up(value, unit):
-    return -(-value // unit) * unit
 
 
 def me_of(ns):
@@ -127,7 +123,7 @@
 
 
 def factor_panels(sums_ref, restart_ref, work, upper, nrows, panel):
-    k, keep = restart_ref.shape
+    keep, k = restart_ref.shape
     width = sums_ref.shape[1]
     row = lax.broadcasted_iota(jnp.int32, (width, width), 0)
     lane = lax.broadcasted_iota(jnp.int32, (width, width), 1)
@@ -159,8 +155,7 @@
         return carry
 
     lax.fori_loop(0, k // panel, step, 0)
-    turned = restart_ref[...].T
-    both = jnp.dot(turned, upper[:k, :], precision=HIGHEST, preferred_element_type=jnp.float32)
+    both = jnp.dot(restart_ref[...], upper[:k, :], precision=HIGHEST, preferred_element_type=jnp.float32)
     half = upper[:, :width].T[k : k + 8, :]
     proj = jnp.dot(half, upper[:, width:], precision=HIGHEST, preferred_element_type=jnp.float32)
     raised = both[:, :k]
@@ -202,7 +197,7 @@
             return carry
         lax.fori_loop(1, ndev, body, 0)
 
-    panel = next(p for p in (4, 2, 1) if restart_ref.shape[0] % p == 0)
+    panel = next(p for p in (4, 2, 1) if restart_ref.shape[1] % p == 0)
     weights, raised = factor_panels(sums_ref, restart_ref, work, upper, nrows, panel)
     load_u.wait()
     load_r.wait()
@@ -253,15 +248,22 @@
     cg[s] = coeff_ref[...]
     for o in range(1, ns):
         coeff_copy((s + o) % ns, (s + o) % ns).wait_recv()
+    deg, mloc, _ = coeff_ref.shape
     turned = [
-        lax.dot_general(raised, cg[t], (((1,), (1,)), ((), ())), precision=HIGHEST,
-                        preferred_element_type=jnp.float32)
-        for t in range(ns)
+        jnp.concatenate(
+            [
+                lax.dot_general(raised, cg[t, i], (((1,), (1,)), ((), ())), precision=HIGHEST,
+                                preferred_element_type=jnp.float32)
+                for t in range(ns)
+            ],
+            axis=1,
+        )
+        for i in range(deg)
     ]
     squares = sum(jnp.sum(part * part) for part in turned)
     scale = lax.rsqrt(jnp.full((1, 1), squares / count + 1e-06, jnp.float32))
-    for t in range(ns):
-        coeff_out[t] = turned[t] * scale
+    for i in range(deg):
+        coeff_out[i] = turned[i] * scale
     own_big.wait()
     own_small.wait()
     loop(lambda j: big_copy(j, j).wait_recv())
@@ -284,7 +286,7 @@
         out_shape=(
             jax.ShapeDtypeStruct((ndev, keep, bs), f32),
             jax.ShapeDtypeStruct((ndev, 2, bs), f32),
-            jax.ShapeDtypeStruct((ns, keep, coeff_t.shape[0]), f32),
+            jax.ShapeDtypeStruct((coeff_t.shape[0], keep, ns * coeff_t.shape[1]), f32),
         ),
         in_specs=[hbm, hbm, vmem, vmem, vmem],
         out_specs=(hbm, hbm, vmem),
@@ -305,8 +307,9 @@
     )(u, r, sums, restart, coeff_t)
 
 
-def place_kernel(ndev, nrows, slots, big, small, rows_out, vec_out, held, in_sem, out_sem):
+def place_kernel(ndev, nrows, slots, big, small_hbm, rows_out, vec_out, held, small, in_sem, out_sem, small_sem):
     bs = held.shape[2]
+    load_small = pltpu.make_async_copy(small_hbm, small, small_sem.at[0])
 
     def fetch(d):
         return pltpu.make_async_copy(big.at[d], held.at[d], in_sem.at[d])
@@ -322,23 +325,26 @@
         lax.fori_loop(0, ndev, body, 0)
 
     loop(lambda d: fetch(d).start())
-    total = jnp.sum(small[:, 1, :], axis=0, keepdims=True)
-    scale = lax.rsqrt(total / nrows + 1e-06)
+    load_small.start()
 
     def move(d):
         fetch(d).wait()
         put(d).start()
+
+    loop(move)
+    load_small.wait()
+    total = jnp.sum(small[:, 1, :], axis=0, keepdims=True)
+    scale = lax.rsqrt(total / nrows + 1e-06)
+    for d in range(ndev):
         cols = pl.ds(pl.multiple_of(slots[0, d] * bs, bs), bs)
         vec_out[:, cols] = small[d, 0:1, :] * scale
-
-    loop(move)
     loop(lambda d: put(d).wait())
 
 
 def place(slot_row, big, small, nrows):
     ndev, keep, bs = big.shape
     vmem = pl.BlockSpec(memory_space=pltpu.VMEM)
-    hbm = pl.BlockSpec(memory_space=pl.ANY)
+    hbm = pl.BlockSpec(memory_space=pltpu.MemorySpace.HBM)
     dma = pltpu.SemaphoreType.DMA((ndev,))
     return pl.pallas_call(
         functools.partial(place_kernel, ndev, nrows),
@@ -346,10 +352,14 @@
             jax.ShapeDtypeStruct((keep, ndev * bs), jnp.float32),
             jax.ShapeDtypeStruct((1, ndev * bs), jnp.float32),
         ),
-        in_specs=[pl.BlockSpec(memory_space=pltpu.SMEM), hbm, vmem],
+        in_specs=[pl.BlockSpec(memory_space=pltpu.SMEM), hbm, hbm],
         out_specs=(hbm, vmem),
-        scratch_shapes=[pltpu.VMEM((ndev, keep, bs), jnp.float32), dma, dma],
-        compiler_params=pltpu.CompilerParams(vmem_limit_bytes=20 * 1024 * 1024),
+        scratch_shapes=[
+            pltpu.VMEM(big.shape, jnp.float32),
+            pltpu.VMEM(small.shape, jnp.float32),
+            dma, dma, pltpu.SemaphoreType.DMA((1,)),
+        ],
+        compiler_params=pltpu.CompilerParams(vmem_limit_bytes=60 * 1024 * 1024),
     )(slot_row, big, small)
 
 
@@ -360,13 +370,9 @@
     nrows = u.shape[1] * ndev
     deg, _, mloc = coeff.shape
     sums = gram_sums(u, r, ndev, ns)
-    coeff_t = coeff.transpose(0, 2, 1).reshape(deg * mloc, k)
-    tall = round_up(deg * mloc, 8)
-    coeff_t = jnp.pad(coeff_t, ((0, tall - deg * mloc), (0, 0)))
-    big, small, turned = exchange(u, r, sums, restart, coeff_t, keep, deg * keep * mloc * ns, ndev, ns)
+    coeff_t = coeff.transpose(0, 2, 1)
+    big, small, new_coeff = exchange(u, r, sums, restart.T, coeff_t, keep, deg * keep * mloc * ns, ndev, ns)
     rows, vec = place(slot_map, big, small, nrows)
-    turned = turned[:, :, : deg * mloc].reshape(ns, keep, deg, mloc)
-    new_coeff = turned.transpose(2, 1, 0, 3).reshape(deg, keep, ns * mloc)
     return rows, vec, new_coeff
 
 

time: 113 us -> 105 us (0.929)
  local copies, waits for them, and re-layouts: 6.62 us -> 0.63 us
  Pallas kernels: 106 us -> 103 us
    unnamed x9 -> x3, local copies, waits for them, and re-layouts: 4.09 us -> 0.63 us
    pallas_call x1, Pallas kernels: 6.8 us -> 4.46 us  [place(): pl.pallas_call(functools.partial(place_kernel, ndev, nrows), out_shape=(j...]
    reshape x2 -> x0, local copies, waits for them, and re-layouts: 1.59 us -> none  [the longest x1 0.8 us: local(): coeff_t = coeff.transpose(0, 2, 1).reshape(deg * mloc, k)]
where the time goes in v3:
time: 105 us; the launch traced here: 104 us
  Pallas kernels  103 us (98%)
    pallas_call x1, Pallas kernels, exchange(): pl.pallas_call(functools.partial(exchange_kernel, ndev, ns, keep, count,...  77.2 us
    pallas_call x1, Pallas kernels, gram_sums(): pl.pallas_call(functools.partial(gram_kernel, ndev, ns, chunk), out_shape...  21.4 us
    pallas_call x1, Pallas kernels, place(): pl.pallas_call(functools.partial(place_kernel, ndev, nrows), out_shape=(j...  4.46 us

profile of v3, /device:TPU:0, one launch (start us, length us, event | category | flops | bytes accessed | tf_op | source)
XLA Modules:
  0.0 104.3 jit_solution(14431577883136751564)
XLA Ops:
  0.6 21.4 %shard_map.76.sums_ref = f32[128,128]{1,0:T(8,128)} custom-call(f32[120,16384]{1,0:T(8,128)} %u_hbm.3, f32[1,16384]{1,0:T(1,128)} %r_hbm.3), custom_call_target="tpu_custom_call" | custom-call | tf_op jit(solution)/shard_map/pallas_call | solution.py:105
  22.0 77.2 %shard_map.77 = (f32[32,40,512]{2,1,0:T(8,128)}, f32[32,2,512]{2,1,0:T(2,128)}, f32[3,40,120]{2,1,0:T(8,128)}) custom-call(f32[120,16384]{1,0:T(8,128)} %u_hbm.3, f32[1,16384]{1,0:T(1,128)} %r_hbm.3, f32[128,128]{1,0:T(8,128)} %shard_map.76.sums_ref, f32[40,120]{1,0:T(8,128)} %bitcast.3, f32[3,30,120]{2,1,0:T(8,128)} %bitcast.2), custom_call_target="tpu_custom_call" | custom-call | tf_op jit(solution)/shard_map/pallas_call | solution.py:284
  99.2 0.0 copy-start
  99.2 4.5 %shard_map.78 = (f32[40,16384]{1,0:T(8,128)}, f32[1,16384]{1,0:T(1,128)}) custom-call(s32[1,32]{1,0:T(1,128)} %slots.1, f32[32,40,512]{2,1,0:T(8,128)} %get-tuple-element.8.big, f32[32,2,512]{2,1,0:T(2,128)} %get-tuple-element.9.small_hbm), custom_call_target="tpu_custom_call" | custom-call | tf_op jit(solution)/shard_map/pallas_call | solution.py:349
  103.7 0.0 copy-done
  103.7 0.6 copy.9
Async XLA Ops:
  99.2 4.5 %copy-start = (f32[3,40,120]{2,1,0:T(8,128)S(1)}, f32[3,40,120]{2,1,0:T(8,128)}, u32[]{:S(2)}) copy-start(f32[3,40,120]{2,1,0:T(8,128)} %get-tuple-element.18) | copy-start | bytes 172804
